TPU v7x, 32 devices: a whole 2x2x4 slice. The times are simulated.
32 devices in a mesh: row: 2 (over x), col: 16 (over z, y, core).
Axes of the slice: x: 2, y: 2, z: 4, core: 2. Of those that a mesh axis runs over, the one named last changes fastest.
Arguments:
- ld_matrix: bfloat16 [32768, 32768], P('row', 'col'), may hold values from -0.23925781 to 0.23925781
- factor: float32 [32768, 256], P(('row', 'col')), may hold values from -0.24 to 0.24
- diag_values: bfloat16 [32768], P('col'), may hold values from 0.5 to 4
Outputs:
- factor_grad: float32 [32768, 256], P(('row', 'col'))
All inputs are finite; a program needn't handle non-finite values.
Results may differ from a plain program's by a relative error of at most 0.003.
Values may be sent and summed in bfloat16 or wider, within the bound.
A program may use at most 128 MiB of HBM per device.

v0:
```python
import math

import jax
import jax.numpy as jnp
from jax import lax
from jax.sharding import PartitionSpec as P


def from_root(value, axis, source):
    kept = jnp.where(lax.axis_index(axis) == source, value, 0).astype(value.dtype)
    return lax.psum(kept, axis)


def local(ld_matrix, factor, diag_values):
    factor_low = factor.astype(jnp.bfloat16)
    row_height = ld_matrix.shape[0]
    col_width = ld_matrix.shape[1]
    rank_width = factor.shape[1]
    row_panel = lax.all_gather(factor_low, "col", axis=0, tiled=True)
    col_index = lax.axis_index("col")
    row_index = lax.axis_index("row")
    per_row = lax.axis_size("col") // lax.axis_size("row")
    offset = col_index % per_row * col_width
    section = lax.dynamic_slice_in_dim(row_panel, offset, col_width, 0)
    col_panel = from_root(section, "row", col_index // per_row)
    diag_float = diag_values.astype(jnp.float32)
    col_ids = col_index * col_width + jnp.arange(col_width, dtype=jnp.int32)
    own_rows = row_height // lax.axis_size("col")
    height = math.gcd(own_rows * lax.axis_size("col"), 512)
    number = own_rows * lax.axis_size("col") // height

    def one_block(number_index):
        first = number_index * height
        ld_block = lax.dynamic_slice_in_dim(ld_matrix, first, height, 0)
        left = lax.dynamic_slice_in_dim(row_panel, first, height, 0)
        row_ids = row_index * row_height + first + jnp.arange(height, dtype=jnp.int32)
        model_part = jnp.dot(left, col_panel.T, preferred_element_type=jnp.float32)
        ondiag = row_ids[:, None] == col_ids[None, :]
        extra = jnp.where(ondiag, diag_float[None, :], jnp.float32(0.0))
        misfit = (model_part + extra - ld_block.astype(jnp.float32)).astype(jnp.bfloat16)
        return 4.0 * jnp.dot(misfit, col_panel, preferred_element_type=jnp.float32)

    blocks = lax.map(one_block, jnp.arange(number, dtype=jnp.int32))
    return lax.psum_scatter(
        blocks.reshape(own_rows * lax.axis_size("col"), rank_width),
        "col",
        scatter_dimension=0,
        tiled=True,
    )


def solution(mesh):
    in_specs = (P("row", "col"), P(("row", "col"), None), P("col"))
    out_specs = P(("row", "col"), None)
    return jax.shard_map(local, mesh=mesh, in_specs=in_specs, out_specs=out_specs, check_vma=False)
```

profile of v0, /device:TPU:0, one launch (start us, length us, event | category | flops | bytes accessed | tf_op | source)
XLA Modules:
  0.0 495.8 jit_solution(5465250970531595996)
XLA Ops:
  8.7 77.8 %all-gather.2.cloned.1.call-done = bf16[16384,256]{1,0:T(8,128)(2,1)} async-done(((bf16[1024,256]{1,0:T(8,128)(2,1)}), bf16[16384,256]{1,0:T(8,128)(2,1)}) %all-gather.2.cloned.1.call-update) | async-done | bytes 8388624 | tf_op jit(solution)/shard_map/all_gather | solution.py:19
  89.7 38.1 %all-reduce.2.cloned.1.call-done = bf16[2048,256]{1,0:T(8,128)(2,1)} async-done(((bf16[2048,256]{1,0:T(8,128)(2,1)}), bf16[2048,256]{1,0:T(8,128)(2,1)}) %all-reduce.2.cloned.1.call-update) | async-done | bytes 1048592 | tf_op jit(solution)/shard_map/psum | solution.py:11
  127.8 183.9 %while.13 = (s32[]{:T(128)}, f32[32,512,256]{2,1,0:T(8,128)}, s32[32]{0:T(128)S(1)}, bf16[16384,256]{1,0:T(8,128)(2,1)}, bf16[2048,256]{1,0:T(8,128)(2,1)}, /*in...) while((s32[]{:T(128)}, f32[32,512,256]{2,1,0:T(8,128)}, ...), condition=%wide.region_2.3_spmd.clone, body=%wide.region_1.2_spmd.clone.sunk | while | flops 1080166912 | bytes 5011147 | solution.py:43
  134.8 4.5 fusion.18
  140.6 4.5 fusion.18
  157.7 4.5 fusion.18
  169.2 4.6 fusion.18
  175.0 4.5 fusion.18
  180.8 4.5 fusion.18
  186.6 4.5 fusion.18
  198.1 4.5 fusion.18
  203.8 4.5 fusion.18
  209.5 4.5 fusion.18
  215.3 4.6 fusion.18
  221.2 4.6 fusion.18
  227.0 4.5 fusion.18
  244.2 4.5 fusion.18
  249.9 4.5 fusion.18
  267.1 4.5 fusion.18
  272.9 4.5 fusion.18
  290.1 4.5 fusion.18
  295.8 4.5 fusion.18
  307.3 4.5 fusion.18
  311.8 177.5 %reduce-scatter.2.cloned.1.call-done = f32[1024,256]{1,0:T(8,128)} async-done(((f32[16384,256]{1,0:T(8,128)}), f32[1024,256]{1,0:T(8,128)}) %reduce-scatter.2.cloned.1.call-update) | async-done | bytes 1048592 | tf_op jit(solution)/shard_map/reduce_scatter | solution.py:44
  (119 shorter events, 77.7 us)
Async XLA Ops:
  6.5 80.0 %all-gather.2.cloned.1.call-start = ((), (), s32[]{:S(2)}) async-start(), calls=%async_computation.1 | async-start | bytes 8912896 | tf_op jit(solution)/shard_map/all_gather | solution.py:19
  8.6 119.2 %all-reduce.2.cloned.1.call-start = ((), (), s32[]{:S(2)}) async-start(), calls=%async_computation.2 | async-start | bytes 2097152 | tf_op jit(solution)/shard_map/psum | solution.py:11
  88.9 400.3 %reduce-scatter.2.cloned.1.call-start = ((), (), s32[]{:S(2)}) async-start(), calls=%async_computation.3 | async-start | bytes 17825792 | tf_op jit(solution)/shard_map/reduce_scatter | solution.py:44
Sparse Core Ops, SparseCore 0:
  9.5 77.0 all-gather.1
  89.1 38.6 all-reduce.1
  311.9 177.3 reduce-scatter.1
where the time goes:
time: 496 us
  waiting for transfers between devices  293 us (59%)
  matrix products  143 us (29%)
  loops' own time  21.6 us (4%)
  local copies, waits for them, and re-layouts  18.6 us (4%)
  between operations  13.1 us (3%)
  other arithmetic  5.51 us (1%)
    reduce_scatter x1, waiting for transfers between devices, local(): lax.psum_scatter(blocks.reshape(own_rows * lax.axis_size('col'), rank_wid...  178 us
    dot_general x32, matrix products, one_block(): return 4.0 * jnp.dot(misfit, col_panel, preferred_element_type=jnp.float32)  143 us
    all_gather x1, waiting for transfers between devices, local(): row_panel = lax.all_gather(factor_low, 'col', axis=0, tiled=True)  77.8 us
    psum x1, waiting for transfers between devices, from_root(): return lax.psum(kept, axis)  38.1 us
    another operation x1, loops' own time, local(): blocks = lax.map(one_block, jnp.arange(number, dtype=jnp.int32))  21.6 us
    dynamic_slice x32, local copies, waits for them, and re-layouts, local(): blocks = lax.map(one_block, jnp.arange(number, dtype=jnp.int32))  18.6 us
  transfers between devices with their start and end apart: 3, of which 3 were waited for; matrix products, arithmetic and copies ran while one was open for 0% of the time, Pallas kernels for 0%

commit v1 on v0

v1 whole, which is shorter than its diff:
```python
import jax
import jax.numpy as jnp
from jax import lax
from jax.sharding import PartitionSpec as P


def local(ld_matrix, factor, diag_values):
    n_row, n_col = lax.axis_size("row"), lax.axis_size("col")
    row_index, col_index = lax.axis_index("row"), lax.axis_index("col")
    factor_low = factor.astype(jnp.bfloat16)
    own, rank = factor.shape
    width = ld_matrix.shape[1]
    panel = jnp.zeros((width, rank), jnp.bfloat16)
    for k in range(n_row):
        pairs = [
            (n_row * c + (r + k) % n_row, r * n_col + c)
            for r in range(n_row)
            for c in range(n_col)
        ]
        piece = lax.ppermute(factor_low, ("row", "col"), pairs)
        at = lax.rem(row_index + k, n_row) * own
        panel = lax.dynamic_update_slice_in_dim(panel, piece, at, 0)
    gram = lax.dot_general(
        factor_low, factor_low, (((0,), (0,)), ((), ())), preferred_element_type=jnp.float32
    )
    gram = lax.psum(gram, ("row", "col"))
    part = jnp.dot(ld_matrix, panel, preferred_element_type=jnp.float32)
    per_row = n_col // n_row
    first = col_index % per_row * width
    scale = jnp.where(row_index == col_index // per_row, diag_values, 0).astype(jnp.float32)
    slab = lax.dynamic_slice_in_dim(part, first, width, 0)
    slab = slab - scale[:, None] * panel.astype(jnp.float32)
    part = lax.dynamic_update_slice_in_dim(part, slab, first, 0).astype(jnp.bfloat16)
    total = lax.psum_scatter(part, "col", scatter_dimension=0, tiled=True)
    model = jnp.dot(factor_low, gram, precision=lax.Precision.HIGHEST, preferred_element_type=jnp.float32)
    return 4.0 * (model - total.astype(jnp.float32))


def solution(mesh):
    in_specs = (P("row", "col"), P(("row", "col"), None), P("col"))
    out_specs = P(("row", "col"), None)
    return jax.shard_map(local, mesh=mesh, in_specs=in_specs, out_specs=out_specs, check_vma=False)
```

time: 496 us -> 221 us (0.45)
  waiting for transfers between devices: 293 us -> 147 us
  matrix products: 143 us -> 34.7 us
  loops' own time: 21.6 us -> 0 us
  local copies, waits for them, and re-layouts: 18.6 us -> 8.77 us
  starting transfers between devices: 0.09 us -> 7.54 us
    reduce_scatter x1, waiting for transfers between devices: 178 us -> 29.7 us  [local(): total = lax.psum_scatter(part, 'col', scatter_dimension=0, tiled=True)]
    dot_general x32 -> x3, matrix products: 143 us -> 34.7 us  [the longest x1 32.1 us: local(): part = jnp.dot(ld_matrix, panel, preferred_element_type=jnp.float32)]
    all_gather x1 -> x0, waiting for transfers between devices: 77.8 us -> none  [local(): row_panel = lax.all_gather(factor_low, 'col', axis=0, tiled=True)]
    psum x1, waiting for transfers between devices: 38.1 us -> 99.7 us  [local(): gram = lax.psum(gram, ('row', 'col'))]
    another operation x1 -> x0, loops' own time: 21.6 us -> none  [local(): blocks = lax.map(one_block, jnp.arange(number, dtype=jnp.int32))]
    dynamic_slice x32 -> x0, local copies, waits for them, and re-layouts: 18.6 us -> none  [local(): blocks = lax.map(one_block, jnp.arange(number, dtype=jnp.int32))]
    ppermute x0 -> x2, waiting for transfers between devices: none -> 17.3 us  [local(): piece = lax.ppermute(factor_low, ('row', 'col'), pairs)]
    ppermute x0 -> x2, starting transfers between devices: none -> 7.49 us  [local(): piece = lax.ppermute(factor_low, ('row', 'col'), pairs)]
  transfers between devices with their start and end apart: 3 -> 4, of which waited for: 3 -> 3; matrix products, arithmetic and copies ran while one was open for 0% -> 21% of each run, Pallas kernels for 0% -> 0%
where the time goes in v1:
time: 221 us; the launch traced here: 220 us
  waiting for transfers between devices  147 us (67%)
  matrix products  34.7 us (16%)
  between operations  14.9 us (7%)
  local copies, waits for them, and re-layouts  8.77 us (4%)
  other arithmetic  7.63 us (3%)
  starting transfers between devices  7.54 us (3%)
    psum x1, waiting for transfers between devices, local(): gram = lax.psum(gram, ('row', 'col'))  99.7 us
    dot_general x1, matrix products, local(): part = jnp.dot(ld_matrix, panel, preferred_element_type=jnp.float32)  32.1 us
    reduce_scatter x1, waiting for transfers between devices, local(): total = lax.psum_scatter(part, 'col', scatter_dimension=0, tiled=True)  29.7 us
    ppermute x2, waiting for transfers between devices, local(): piece = lax.ppermute(factor_low, ('row', 'col'), pairs)  17.3 us
    ppermute x2, starting transfers between devices, local(): piece = lax.ppermute(factor_low, ('row', 'col'), pairs)  7.49 us
    unnamed x2, local copies, waits for them, and re-layouts  7.26 us
  transfers between devices with their start and end apart: 4, of which 3 were waited for; matrix products, arithmetic and copies ran while one was open for 21% of the time, Pallas kernels for 0%

profile of v1, /device:TPU:0, one launch (start us, length us, event | category | flops | bytes accessed | tf_op | source)
XLA Modules:
  0.0 220.3 jit_solution(2321519786538181490)
XLA Ops:
  7.4 0.0 all-reduce.2.cloned.1.call-start
  7.4 1.4 copy.4
  8.8 0.7 collective-permute-start
  9.5 6.8 %collective-permute-start.1 = (bf16[1024,256]{0,1:T(8,128)(2,1)S(1)}, bf16[1024,256]{0,1:T(8,128)(2,1)S(1)}, u32[]{:S(2)}, u32[]{:S(2)}) collective-permute-start(bf16[1024,256]{0,1:T(8,128)(2,1)S(1)} %copy.4), channel_id=1, source_target_pairs={{1,0},{3,1},{5,2},{7,3},{9,4},{11,5},{13,6},{15,7},{17,8},{19,9},{... | collective-permute-start | bytes 1572872 | tf_op jit(solution)/shard_map/ppermute | solution.py:20
  16.3 1.0 fusion.1
  17.3 0.0 all-reduce.2.cloned.1.call-update
  17.4 0.0 reduce-scatter.2.cloned.1.call-start
  17.5 0.7 select_convert_fusion
  18.2 0.0 collective-permute-done
  18.2 0.1 broadcast_in_dim.8
  18.3 0.1 constant_dynamic-update-slice_fusion.1
  18.3 17.3 %collective-permute-done.1 = bf16[1024,256]{0,1:T(8,128)(2,1)S(1)} collective-permute-done((bf16[1024,256]{0,1:T(8,128)(2,1)S(1)}, bf16[1024,256]{0,1:T(8,128)(2,1)S(1)}, u32[]{:S(2)}, u32[]{:S(2)}) %collective-permute-start.1) | collective-permute-done | bytes 524320 | tf_op jit(solution)/shard_map/ppermute | solution.py:20
  35.7 32.1 %fusion.2 = f32[256,16384]{1,0:T(8,128)} fusion(bf16[2048,256]{0,1:T(8,128)(2,1)S(1)} %constant_dynamic-update-slice_fusion, bf16[16384,2048]{1,0:T(8,128)(2,1)} %param.3), kind=kOutput, calls=%fused_computation.8 | convolution fusion | flops 17179869184 | bytes 84934656 | tf_op jit(solution)/shard_map/dot_general | solution.py:27
  67.8 5.8 %copy.9 = f32[16384,256]{0,1:T(8,128)S(1)} copy(f32[16384,256]{0,1:T(8,128)} %bitcast.13) | data formatting | bytes 33554432
  73.7 2.0 fusion
  75.7 3.7 %convert_element_type.20 = bf16[16384,256]{0,1:T(8,128)(2,1)} convert(f32[16384,256]{0,1:T(8,128)S(1)} %fusion) | non-fusion elementwise | flops 4194304 | bytes 25165824 | tf_op jit(solution)/shard_map/convert_element_type | solution.py:33
  79.4 0.0 reduce-scatter.2.cloned.1.call-update
  79.5 99.7 %all-reduce.2.cloned.1.call-done = f32[256,256]{1,0:T(8,128)} async-done(((f32[256,256]{1,0:T(8,128)}), f32[256,256]{1,0:T(8,128)}) %all-reduce.2.cloned.1.call-update) | async-done | bytes 262160 | tf_op jit(solution)/shard_map/psum | solution.py:26
  179.1 1.6 convolution_bitcast_fusion
  180.7 29.7 %reduce-scatter.2.cloned.1.call-done = bf16[1024,256]{0,1:T(8,128)(2,1)} async-done(((bf16[16384,256]{0,1:T(8,128)(2,1)}), bf16[1024,256]{0,1:T(8,128)(2,1)}) %reduce-scatter.2.cloned.1.call-update) | async-done | bytes 524304 | tf_op jit(solution)/shard_map/reduce_scatter | solution.py:34
  210.4 1.2 subtract_multiply_fusion
  211.6 1.3 copy.5
  (1 shorter events, 0.0 us)
Async XLA Ops:
  7.4 171.8 %all-reduce.2.cloned.1.call-start = ((), (), s32[]{:S(2)}) async-start(), calls=%async_computation.1 | async-start | bytes 524288 | tf_op jit(solution)/shard_map/psum | solution.py:26
  8.8 9.4 %collective-permute-start = (bf16[1024,256]{0,1:T(8,128)(2,1)S(1)}, bf16[1024,256]{0,1:T(8,128)(2,1)S(1)}, u32[]{:S(2)}, u32[]{:S(2)}) collective-permute-start(bf16[1024,256]{0,1:T(8,128)(2,1)S(1)} %copy.4), channel_id=1, source_target_pairs={{0,0},{2,1},{4,2},{6,3},{8,4},{10,5},{12,6},{14,7},{16,8},{18,9},{... | collective-permute-start | bytes 1572872 | tf_op jit(solution)/shard_map/ppermute | solution.py:20
  9.5 26.1 %collective-permute-start.1 = (bf16[1024,256]{0,1:T(8,128)(2,1)S(1)}, bf16[1024,256]{0,1:T(8,128)(2,1)S(1)}, u32[]{:S(2)}, u32[]{:S(2)}) collective-permute-start(bf16[1024,256]{0,1:T(8,128)(2,1)S(1)} %copy.4), channel_id=1, source_target_pairs={{1,0},{3,1},{5,2},{7,3},{9,4},{11,5},{13,6},{15,7},{17,8},{19,9},{... | collective-permute-start | bytes 1572872 | tf_op jit(solution)/shard_map/ppermute | solution.py:20
  17.4 193.0 %reduce-scatter.2.cloned.1.call-start = ((), (), s32[]{:S(2)}) async-start(), calls=%async_computation.2 | async-start | bytes 8912896 | tf_op jit(solution)/shard_map/reduce_scatter | solution.py:34
Sparse Core Ops, SparseCore 0:
  17.5 161.5 all-reduce.1
Sparse Core Ops, SparseCore 1:
  79.5 130.8 reduce-scatter.1
